TPU v7x, 256 devices: a whole 4x4x8 slice. The times are simulated.
256 devices in a mesh: seq: 32 (over y, z), head: 8 (over x, core).
Axes of the slice: x: 4, y: 4, z: 8, core: 2. Of those that a mesh axis runs over, the one named last changes fastest.
Arguments:
- tokens: bfloat16 [24576, 2560], P(('seq', 'head')), may hold values from -12 to 12
- pre_gain: float32 [2560], replicated, may hold values from 0.25 to 1.75
- inner_proj: bfloat16 [2560, 2, 5120], P(None, None, 'head'), may hold values from -0.125 to 0.125
- outer_proj: bfloat16 [2560, 336], replicated, may hold values from -0.125 to 0.125
- kernel_x: float32 [4, 5120], P(None, 'head'), may hold values from -3 to 3
- kernel_bc: float32 [4, 256], replicated, may hold values from -3 to 3
- offset_x: float32 [5120], P('head'), may hold values from -3 to 3
- offset_bc: float32 [256], replicated, may hold values from -3 to 3
- dt_bias: float32 [80], P('head'), may hold values from -7 to -5
- a_log: float32 [80], P('head'), may hold values from -12 to 4
- skip_gain: float32 [80], P('head'), may hold values from 0.5 to 1.5
- norm_gain: float32 [5120], P('head'), may hold values from 0.25 to 1.75
- out_proj: bfloat16 [5120, 2560], P('head'), may hold values from -0.078125 to 0.078125
Outputs:
- mixed: bfloat16 [24576, 2560], P(('seq', 'head'))
All inputs are finite; a program needn't handle non-finite values.
Results may differ from a plain program's by a relative error of at most 0.014.
Values may be sent and summed in bfloat16 or wider, within the bound.
A program may use at most 128 MiB of HBM per device.

v0:
```python
import jax
import jax.numpy as jnp
from jax import lax
from jax.sharding import Mesh
from jax.sharding import PartitionSpec as P

SPAN = 256
SEQ = ("seq_0", "seq_1")
SEQ_HEAD = ("seq_0", "seq_1", "head")
norm_floor = 0.1


def passed_along(block, axis, distance):
    devices = range(lax.axis_size(axis))
    route = [(i - distance, i) for i in devices if i - distance in devices]
    return lax.ppermute(block, axis, route)


def nothing_yet(array, identity):
    return jax.tree.map(
        lambda part, zero: jnp.zeros_like(part) + jnp.asarray(zero, part.dtype), array, identity
    )


def entering(array, axes, combine, identity):
    before = start = nothing_yet(array, identity)
    subtotal = array
    for axis in reversed(axes):
        length, position = (lax.axis_size(axis), lax.axis_index(axis))
        pieces = jax.tree.map(
            lambda part, kind: lax.all_gather(part.astype(kind), axis),
            subtotal,
            (jnp.bfloat16, jnp.bfloat16),
        )
        inside, subtotal = (start, start)
        for k in range(length):
            passed = k < position
            subtotal = combine(
                subtotal, jax.tree.map(lambda part, own: part[k].astype(own.dtype), pieces, array)
            )
            inside = jax.tree.map(lambda new, old: jnp.where(passed, new, old), subtotal, inside)
        before = combine(inside, before)
    return before


def from_everyone(array, axis):
    length = lax.axis_size(axis)
    return lax.all_to_all(
        jnp.broadcast_to(array[None], (length, *array.shape)), axis, 0, 0, tiled=True
    )


def taken_together(array, axis):
    everything = from_everyone(array, axis)
    return jnp.sum(everything, axis=0)


def cut_along(array, dim, length):
    before, after = (array.shape[:dim], array.shape[dim + 1 :])
    return jnp.moveaxis(array.reshape(*before, length, -1, *after), dim, 0)


def summed_on_arrival(array, axis, dim):
    pieces = cut_along(array, dim, lax.axis_size(axis))
    arrived = lax.all_to_all(pieces, axis, split_axis=0, concat_axis=0, tiled=True)
    return arrived.astype(jnp.float32).sum(axis=0)


def row_norm(row_block, gain_vector):
    widened = row_block.astype(jnp.float32)
    inverse_rms = lax.rsqrt(jnp.mean(widened * widened, axis=-1, keepdims=True) + norm_floor)
    return widened * inverse_rms * gain_vector


def masked_exp(log_gap, causal):
    return jnp.where(causal, jnp.exp(jnp.where(causal, log_gap, 0.0)), 0.0)


def on_device(
    tokens,
    pre_gain,
    inner_proj,
    outer_proj,
    kernel_x,
    kernel_bc,
    offset_x,
    offset_bc,
    dt_bias,
    a_log,
    skip_gain,
    norm_gain,
    out_proj,
):
    model_width = inner_proj.shape[0]
    local_width = inner_proj.shape[2]
    head_count = dt_bias.shape[0]
    head_size = local_width // head_count
    state_size = kernel_bc.shape[1] // 2
    kernel_size = kernel_x.shape[0]
    joined_proj = inner_proj.reshape(model_width, 2 * local_width)
    own_normed = row_norm(tokens, pre_gain).astype(jnp.bfloat16)
    normed = lax.all_gather(own_normed, "head", axis=0, tiled=True)
    inner_part = jnp.dot(normed, joined_proj, preferred_element_type=jnp.float32)
    outer_part = jnp.dot(normed, outer_proj, preferred_element_type=jnp.float32)
    projected = jnp.concatenate([inner_part, outer_part], axis=1)
    seq_rows = projected.shape[0]
    gate_in = projected[:, :local_width].astype(jnp.bfloat16)
    conv_input = projected[:, local_width : 2 * local_width + 2 * state_size].astype(jnp.bfloat16)
    head_index = lax.axis_index("head")
    dt_raw = lax.dynamic_slice_in_dim(
        projected[:, 2 * local_width + 2 * state_size :], head_index * head_count, head_count, 1
    )
    conv_tail = passed_along(conv_input[seq_rows - kernel_size + 1 :], SEQ, 1)
    extended = jnp.concatenate([conv_tail, conv_input], axis=0)
    conv_weight = jnp.concatenate([kernel_x, kernel_bc], axis=1)
    conv_bias = jnp.concatenate([offset_x, offset_bc])
    summed = jnp.broadcast_to(conv_bias, conv_input.shape)
    for offset in range(kernel_size):
        summed = summed + conv_weight[offset] * extended[offset : offset + seq_rows].astype(
            jnp.float32
        )
    conv_out = jax.nn.silu(summed).astype(jnp.bfloat16)
    blocks = seq_rows // SPAN
    values_x = conv_out[:, :local_width].reshape(blocks, SPAN, head_count, head_size)
    values_b = conv_out[:, local_width : local_width + state_size].reshape(blocks, SPAN, state_size)
    values_c = conv_out[:, local_width + state_size :].reshape(blocks, SPAN, state_size)
    step_flat = jax.nn.softplus(dt_raw + dt_bias)
    log_rates = (step_flat * -jnp.exp(a_log)).reshape(blocks, SPAN, head_count)
    step_sizes = step_flat.reshape(blocks, SPAN, head_count)
    running = jnp.cumsum(log_rates, axis=1)
    score_rows = jnp.einsum("ctn,csn->cts", values_c, values_b, preferred_element_type=jnp.float32)
    running_heads = jnp.transpose(running, (0, 2, 1))
    steps_heads = jnp.transpose(step_sizes, (0, 2, 1))
    row_index = lax.broadcasted_iota(jnp.int32, (SPAN, SPAN), 0)
    col_index = lax.broadcasted_iota(jnp.int32, (SPAN, SPAN), 1)
    decay_factor = masked_exp(
        running_heads[:, :, :, None] - running_heads[:, :, None, :], row_index >= col_index
    )
    mix_weights = (score_rows[:, None] * decay_factor * steps_heads[:, :, None, :]).astype(
        jnp.bfloat16
    )
    intra_out = jnp.einsum(
        "chts,cshp->cthp", mix_weights, values_x, preferred_element_type=jnp.float32
    )
    end_weight = jnp.exp(running[:, -1:, :] - running) * step_sizes
    scaled_x = (values_x.astype(jnp.float32) * end_weight[..., None]).astype(jnp.bfloat16)
    block_states = jnp.einsum(
        "cshp,csn->chpn", scaled_x, values_b, preferred_element_type=jnp.float32
    )
    block_total = running[:, -1, :]
    prefix_rate = jnp.concatenate(
        [jnp.zeros((1, head_count), jnp.float32), jnp.cumsum(block_total, axis=0)], axis=0
    )
    prefix_heads = prefix_rate.T
    later_index = lax.broadcasted_iota(jnp.int32, (blocks + 1, blocks), 0)
    source_index = lax.broadcasted_iota(jnp.int32, (blocks + 1, blocks), 1)
    link_weight = masked_exp(
        prefix_heads[:, :, None] - prefix_heads[:, None, 1:], source_index < later_index
    )
    local_states = jnp.einsum(
        "hce,ehpn->chpn", link_weight, block_states, precision=lax.Precision.HIGHEST
    )
    summary = local_states[blocks]
    device_rate = prefix_rate[blocks]

    def combine(earlier_part, later_part):
        return (
            earlier_part[0] + later_part[0],
            jnp.exp(later_part[0])[:, None, None] * earlier_part[1] + later_part[1],
        )

    identity = (
        jnp.zeros((head_count,), jnp.float32),
        jnp.zeros((head_count, head_size, state_size), jnp.float32),
    )
    carried = entering((device_rate, summary), SEQ, combine, identity)[1]
    block_inputs = (
        local_states[:blocks] + jnp.exp(prefix_rate[:blocks])[:, :, None, None] * carried[None]
    )
    cross_out = jnp.exp(running)[..., None] * jnp.einsum(
        "ctn,chpn->cthp",
        values_c.astype(jnp.float32),
        block_inputs,
        precision=lax.Precision.HIGHEST,
    )
    mixer_out = (intra_out + cross_out + skip_gain[:, None] * values_x.astype(jnp.float32)).reshape(
        seq_rows, local_width
    )
    gated = mixer_out * jax.nn.silu(gate_in.astype(jnp.float32))
    squares = taken_together(jnp.sum(gated * gated, axis=1), "head")
    inverse_rms = lax.rsqrt(squares / (local_width * lax.axis_size("head")) + norm_floor)
    normed_out = (gated * inverse_rms[:, None] * norm_gain).astype(jnp.bfloat16)
    mixed = summed_on_arrival(
        jnp.dot(normed_out, out_proj, preferred_element_type=jnp.float32).astype(jnp.bfloat16),
        "head",
        0,
    )
    return mixed.astype(jnp.bfloat16)


def solution(mesh):
    finer = Mesh(mesh.devices.reshape(4, 8, mesh.shape["head"]), ("seq_0", "seq_1", "head"))
    in_specs = (
        P(SEQ_HEAD, None),
        P(),
        P(None, None, "head"),
        P(),
        P(None, "head"),
        P(),
        P("head"),
        P(),
        P("head"),
        P("head"),
        P("head"),
        P("head"),
        P("head", None),
    )
    out_specs = P(SEQ_HEAD, None)
    return jax.shard_map(
        on_device, mesh=finer, in_specs=in_specs, out_specs=out_specs, check_vma=False
    )
```

profile of v0, /device:TPU:1, one launch (start us, length us, event | category | flops | bytes accessed | tf_op | source)
XLA Modules:
  0.0 240.8 jit_solution(7252940572213324971)
XLA Ops:
  6.5 1.4 fusion.16
  7.9 2.0 fusion.18
  10.1 6.7 %copy.137 = bf16[320,8,2,640]{3,1,2,0:T(8,128)(2,1)} copy(bf16[320,8,2,640]{3,2,1,0:T(2,128)(2,1)} %bitcast.167) | data formatting | bytes 13107200
  16.8 0.6 iota_compare_fusion.1
  17.4 0.6 pad_maximum_fusion.3
  18.1 29.7 %all-gather.5.cloned.1.call-done = bf16[768,2560]{1,0:T(8,128)(2,1)} async-done(((bf16[96,2560]{1,0:T(8,128)(2,1)}), bf16[768,2560]{1,0:T(8,128)(2,1)}) %all-gather.5.cloned.1.call-update) | async-done | bytes 3932176 | tf_op jit(solution)/shard_map/all_gather | solution.py:102
  47.8 5.3 %fusion.66 = (bf16[768,336]{0,1:T(8,128)(2,1)}, f32[768,336]{0,1:T(8,128)}) fusion(bf16[768,2560]{1,0:T(8,128)(2,1)} %all-gather.5.cloned.1.call-done, bf16[2560,336]{0,1:T(8,128)(2,1)} %param.16), kind=kOutput, calls=%fused_computation.144 | convolution fusion | flops 1321463808 | bytes 7200768 | tf_op jit(solution)/shard_map/dot_general | solution.py:104
  53.1 2.1 copy.111
  55.2 8.9 %convolution_convert_fusion.1 = bf16[768,1280]{1,0:T(8,128)(2,1)S(1)} fusion(bf16[768,2560]{1,0:T(8,128)(2,1)} %all-gather.5.cloned.1.call-done, bf16[2560,1280]{1,0:T(8,128)(2,1)} %bitcast.168), kind=kOutput, calls=%fused_computation.9 | convolution fusion | flops 5034147840 | bytes 12451840 | tf_op jit(solution)/shard_map/dot_general | solution.py:103
  64.2 1.3 pad_maximum_fusion.1
  65.5 0.4 copy-done.1
  65.9 0.6 pad_maximum_fusion.2
  66.5 1.0 slice.213
  67.4 0.1 broadcast_multiply_fusion
  67.6 1.7 reduce-window.6
  69.3 0.2 slice_reduce_fusion
  69.6 0.1 broadcast_add_fusion
  69.8 0.1 copy.121
  69.9 0.1 copy.122
  70.1 3.2 %collective-permute-start = (bf16[3,896]{1,0:T(4,128)(2,1)}, bf16[3,896]{1,0:T(4,128)(2,1)S(1)}, u32[]{:S(2)}, u32[]{:S(2)}) collective-permute-start(bf16[3,896]{1,0:T(4,128)(2,1)} %pad_maximum_fusion.2), channel_id=1, source_target_pairs={{0,8},{8,16},{16,24},{24,32},{32,40},{40,48},{48,56},{56,64},{64,7... | collective-permute-start | bytes 16136 | tf_op jit(solution)/shard_map/ppermute | solution.py:16
  73.3 0.6 bitcast_exponential_fusion
  73.9 0.7 copy.124
  74.6 0.6 copy.123
  75.2 0.7 copy.125
  75.9 5.0 %multiply_convert_fusion.2 = bf16[768,896]{1,0:T(8,128)(2,1)S(1)} fusion(bf16[768,896]{1,0:T(8,128)(2,1)} %pad_maximum_fusion.1, bf16[3,896]{1,0:T(4,128)(2,1)S(1)} %collective-permute-done, f32[896]{0:T(1024)S(1)} %get-tuple-element.6, f32[896]{0:T(1024)S(1)} %get-tuple-element.7, f32[896]{0:T(1024)S(1)} %get-tuple-element.8, f32[896]{0:T(1024)S(1)} %get-tuple-element.5, ...), kind=kLoop, calls=%fused_computation.10 | loop fusion | flops 17891328 | bytes 2775808 | tf_op jit(solution)/shard_map/convert_element_type | solution.py:122
  80.9 0.7 fusion.65
  81.6 1.1 slice.210
  82.6 2.3 copy.112
  84.9 3.8 %reshape.237 = bf16[3,256,10,64]{1,0,3,2:T(4,128)(2,1)} reshape(bf16[768,640]{0,1:T(8,128)(2,1)} %copy.112) | data formatting | bytes 1966080 | tf_op jit(solution)/shard_map/reshape | solution.py:124
  88.7 1.8 fusion.19
  90.5 2.8 %convolution_bitcast_fusion = f32[4,10,64,128]{3,0,2,1:T(4,128)S(1)} fusion(f32[3,10,64,128]{3,2,1,0:T(8,128)S(1)} %fusion.19, f32[10,3]{1,0:T(8,128)S(1)} %copy-done.14, f32[10,4]{1,0:T(8,128)S(1)} %copy-done.13, pred[4,3]{1,0:T(4,128)(4,1)S(1)} %copy-done.27), kind=kOutput, calls=%fused_computation.26 | convolution fusion | flops 11796840 | bytes 2294052 | tf_op jit(solution)/shard_map/hce,ehpn->chpn/dot_general | solution.py:160
  93.4 1.1 copy-done.2
  94.4 0.3 slice.387
  94.8 0.7 copy.128
  95.5 0.6 iota_compare_fusion
  96.2 1.4 slice_exponential_fusion
  97.5 12.2 %all-gather = bf16[8,1,10]{2,1,0:T(2,128)(2,1)S(1)} all-gather(bf16[1,1,10]{2,1,0:T(2,128)(2,1)S(1)} %slice_bitcast_fusion.5), channel_id=1, replica_groups=mesh['seq_0'=4,'seq_1'=8,'head'=8] {'seq_1'}, dimensions={0}, use_global_device_ids=true | all-gather | bytes 180 | tf_op jit(solution)/shard_map/all_gather | solution.py:31
  109.7 0.6 fusion.39
  110.3 0.6 convert_bitcast_fusion
  110.9 8.6 %all-gather.1 = bf16[4,1,10]{2,1,0:T(2,128)(2,1)} all-gather(bf16[1,1,10]{2,1,0:T(2,128)(2,1)S(1)} %get-tuple-element.17), channel_id=1, replica_groups=mesh['seq_0'=4,'seq_1'=8,'head'=8] {'seq_0'}, dimensions={0}, use_global_device_ids=true | all-gather | bytes 100 | tf_op jit(solution)/shard_map/all_gather | solution.py:31
  119.5 0.6 copy.115
  120.2 0.8 copy.127
  120.9 1.4 copy.119
  122.3 0.6 copy.117
  123.0 0.6 exponential_bitcast_fusion
  123.6 0.7 fusion.49
  124.3 2.1 fusion.67
  126.4 4.1 %all-gather.7.cloned.1.call-done = bf16[8,10,64,128]{3,2,1,0:T(8,128)(2,1)} async-done(((bf16[1,10,64,128]{3,2,1,0:T(8,128)(2,1)}), bf16[8,10,64,128]{3,2,1,0:T(8,128)(2,1)}) %all-gather.7.cloned.1.call-update) | async-done | bytes 1310736 | tf_op jit(solution)/shard_map/all_gather | solution.py:31
  130.4 1.9 fusion.28
  132.3 10.4 %all_gather.23 = bf16[4,10,64,128]{3,2,1,0:T(8,128)(2,1)S(1)} all-gather(bf16[1,10,64,128]{3,2,1,0:T(8,128)(2,1)S(1)} %fusion.28), channel_id=1, replica_groups=mesh['seq_0'=4,'seq_1'=8,'head'=8] {'seq_0'}, dimensions={0}, use_global_device_ids=true | all-gather | bytes 819200 | tf_op jit(solution)/shard_map/all_gather | solution.py:31
  142.8 1.0 add_bitcast_fusion
  143.8 0.4 slice_add_fusion
  144.3 0.9 fusion.21
  145.2 0.3 copy-done.6
  145.5 0.2 copy-done.7
  145.7 2.7 %fusion.8 = f32[3,256,10,64]{1,3,2,0:T(8,128)S(1)} fusion(f32[3,256,10,64]{1,3,2,0:T(8,128)S(1)} %fusion.21, f32[3,10,256]{2,1,0:T(8,128)S(1)} %copy-done.11, f32[3,10,256]{2,1,0:T(8,128)S(1)} %copy-done.9, f32[3,256,256]{2,1,0:T(8,128)S(1)} %copy-done.7, pred[256,256]{1,0:T(8,128)(4,1)S(1)} %copy-done.8, f32[10]{0:T(128)S(1)} %copy-done.30, ...), kind=kOutput, calls=%fused_computation.16 | convolution fusion | flops 265912320 | bytes 5859368 | tf_op jit(solution)/shard_map/chts,cshp->cthp/dot_general | solution.py:142
  148.4 1.4 copy.130
  149.8 1.8 copy.138
  151.6 2.8 %copy.131 = f32[768,640]{1,0:T(8,128)} copy(f32[768,640]{0,1:T(8,128)} %bitcast.166) | data formatting | bytes 3932160 | tf_op jit(solution)/shard_map/reshape | solution.py:186
  154.4 2.5 %multiply_reduce_fusion = f32[768]{0:T(1024)S(1)} fusion(f32[768,640]{1,0:T(8,128)} %copy.131, bf16[768,1280]{1,0:T(8,128)(2,1)} %copy-done.1), kind=kLoop, calls=%fused_computation.23 | loop fusion | flops 3931392 | bytes 2952192 | tf_op jit(solution)/shard_map/reduce_sum | solution.py:190
  156.9 17.4 %all_to_all.11 = f32[8,1,768]{2,1,0:T(1,128)S(1)} all-to-all(f32[8,1,768]{2,1,0:T(1,128)S(1)} %broadcast_in_dim.36), channel_id=1, replica_groups=mesh['seq_0'=4,'seq_1'=8,'head'=8] {'head'}, dimensions={0} | all-to-all | bytes 49152 | tf_op jit(solution)/shard_map/all_to_all | solution.py:48
  174.4 6.2 %convolution_convert_fusion = bf16[768,2560]{1,0:T(8,128)(2,1)S(1)} fusion(bf16[640,2560]{1,0:T(8,128)(2,1)S(1)} %copy-done, f32[640]{0:T(1024)S(1)} %copy-done.28, f32[768]{0:T(1024)S(1)} %add_rsqrt_fusion, f32[768,640]{1,0:T(8,128)} %copy.131, bf16[768,1280]{1,0:T(8,128)(2,1)} %copy-done.1), kind=kOutput, calls=%fused_computation.1 | convolution fusion | flops 2522972160 | bytes 10163712 | tf_op jit(solution)/shard_map/dot_general | solution.py:194
  180.6 49.8 %all_to_all.12 = bf16[8,96,2560]{2,1,0:T(8,128)(2,1)} all-to-all(bf16[8,96,2560]{2,1,0:T(8,128)(2,1)S(1)} %bitcast.169), channel_id=1, replica_groups=mesh['seq_0'=4,'seq_1'=8,'head'=8] {'head'}, dimensions={0} | all-to-all | bytes 7864320 | tf_op jit(solution)/shard_map/all_to_all | solution.py:65
  230.4 3.6 %reduce_sum.42 = bf16[96,2560]{1,0:T(8,128)(2,1)} reduce(bf16[8,96,2560]{2,1,0:T(8,128)(2,1)} %all_to_all.12, bf16[]{:T(256)} %constant.60.clone.1), dimensions={0}, to_apply=%region_6.7 | reduce | flops 1720320 | bytes 4423682 | tf_op jit(solution)/shard_map/reduce_sum | solution.py:66
  (84 shorter events, 0.6 us)
Async XLA Ops:
  6.5 167.9 %copy-start = (bf16[640,2560]{1,0:T(8,128)(2,1)S(1)}, bf16[640,2560]{1,0:T(8,128)(2,1)}, u32[]{:S(2)}) copy-start(bf16[640,2560]{1,0:T(8,128)(2,1)} %param.25) | copy-start | bytes 9830404
  6.5 41.2 %all-gather.5.cloned.1.call-start = ((), (), s32[]{:S(2)}) async-start(), calls=%async_computation.2 | async-start | bytes 4423680 | tf_op jit(solution)/shard_map/all_gather | solution.py:102
  10.0 120.5 %all-gather.7.cloned.1.call-start = ((), (), s32[]{:S(2)}) async-start(), calls=%async_computation.3 | async-start | bytes 1474560 | tf_op jit(solution)/shard_map/all_gather | solution.py:31
  10.0 7.4 %copy-start.16 = (f32[4,640]{1,0:T(4,128)S(1)}, f32[4,640]{1,0:T(4,128)}, u32[]{:S(2)}) copy-start(f32[4,640]{1,0:T(4,128)} %param.17) | copy-start | bytes 30724
  10.0 7.4 %copy-start.22 = (f32[4,256]{1,0:T(4,128)S(1)}, f32[4,256]{1,0:T(4,128)}, u32[]{:S(2)}) copy-start(f32[4,256]{1,0:T(4,128)} %param.18) | copy-start | bytes 12292
  10.0 7.4 %copy-start.23 = (f32[640]{0:T(1024)S(1)}, f32[640]{0:T(1024)}, u32[]{:S(2)}) copy-start(f32[640]{0:T(1024)} %param.19) | copy-start | bytes 7684
  10.1 7.4 %copy-start.25 = (f32[256]{0:T(256)S(1)}, f32[256]{0:T(256)}, u32[]{:S(2)}) copy-start(f32[256]{0:T(256)} %param.20) | copy-start | bytes 3076
  10.1 8.0 %copy-start.29 = (f32[10]{0:T(128)S(1)}, f32[10]{0:T(128)}, u32[]{:S(2)}) copy-start(f32[10]{0:T(128)} %param.22) | copy-start | bytes 124
  55.2 8.9 %copy-start.4 = (bf16[768,336]{1,0:T(8,128)(2,1)S(1)}, bf16[768,336]{1,0:T(8,128)(2,1)}, u32[]{:S(2)}) copy-start(bf16[768,336]{1,0:T(8,128)(2,1)} %copy.111) | copy-start | bytes 1548292
  64.2 1.7 copy-start.1
  65.9 1.6 copy-start.26
  70.0 5.9 %copy-start.15 = (f32[3,10]{1,0:T(4,128)}, f32[3,10]{1,0:T(4,128)S(1)}, u32[]{:S(2)}) copy-start(f32[3,10]{1,0:T(4,128)S(1)} %reduce_window_sum.36) | copy-start | bytes 364
  70.1 5.8 %collective-permute-start = (bf16[3,896]{1,0:T(4,128)(2,1)}, bf16[3,896]{1,0:T(4,128)(2,1)S(1)}, u32[]{:S(2)}, u32[]{:S(2)}) collective-permute-start(bf16[3,896]{1,0:T(4,128)(2,1)} %pad_maximum_fusion.2), channel_id=1, source_target_pairs={{0,8},{8,16},{16,24},{24,32},{32,40},{40,48},{48,56},{56,64},{64,7... | collective-permute-start | bytes 16136 | tf_op jit(solution)/shard_map/ppermute | solution.py:16
  88.7 1.8 copy-start.13
  88.7 1.8 copy-start.14
  88.7 1.8 copy-start.27
  93.4 1.1 copy-start.2
  109.7 10.4 %copy-start.12 = (bf16[8,1,10]{2,1,0:T(2,128)(2,1)}, bf16[8,1,10]{2,1,0:T(2,128)(2,1)S(1)}, u32[]{:S(2)}) copy-start(bf16[8,1,10]{2,1,0:T(2,128)(2,1)S(1)} %all-gather) | copy-start | bytes 484
  120.1 22.6 %copy-start.17 = (f32[10]{0:T(128)S(1)}, f32[10]{0:T(128)}, u32[]{:S(2)}) copy-start(f32[10]{0:T(128)} %get-tuple-element.18) | copy-start | bytes 124
  120.1 22.6 %copy-start.18 = (f32[10]{0:T(128)S(1)}, f32[10]{0:T(128)}, u32[]{:S(2)}) copy-start(f32[10]{0:T(128)} %get-tuple-element.19) | copy-start | bytes 124
  120.1 22.6 %copy-start.19 = (f32[10]{0:T(128)S(1)}, f32[10]{0:T(128)}, u32[]{:S(2)}) copy-start(f32[10]{0:T(128)} %get-tuple-element.20) | copy-start | bytes 124
  120.1 22.6 %copy-start.20 = (f32[10]{0:T(128)S(1)}, f32[10]{0:T(128)}, u32[]{:S(2)}) copy-start(f32[10]{0:T(128)} %get-tuple-element.21) | copy-start | bytes 124
  120.2 22.6 %copy-start.21 = (f32[10]{0:T(128)S(1)}, f32[10]{0:T(128)}, u32[]{:S(2)}) copy-start(f32[10]{0:T(128)} %get-tuple-element.22) | copy-start | bytes 124
  123.0 19.8 %copy-start.24 = (f32[10]{0:T(128)S(1)}, f32[10]{0:T(128)}, u32[]{:S(2)}) copy-start(f32[10]{0:T(128)} %get-tuple-element.9) | copy-start | bytes 124
  130.4 12.3 %copy-start.5 = (bf16[8,10,64,128]{3,2,1,0:T(8,128)(2,1)S(1)}, bf16[8,10,64,128]{3,2,1,0:T(8,128)(2,1)}, u32[]{:S(2)}) copy-start(bf16[8,10,64,128]{3,2,1,0:T(8,128)(2,1)} %all-gather.7.cloned.1.call-done) | copy-start | bytes 3932164
  130.4 13.3 %copy-start.3 = (f32[4,10,64,128]{3,0,2,1:T(4,128)S(1)}, f32[4,10,64,128]{3,0,2,1:T(4,128)}, u32[]{:S(2)}) copy-start(f32[4,10,64,128]{3,0,2,1:T(4,128)} %copy-done.2) | copy-start | bytes 3932164
  144.2 1.3 copy-start.6
  144.2 1.5 copy-start.7
  144.2 1.5 copy-start.8
  144.2 1.5 copy-start.9
  144.2 1.5 copy-start.10
  144.2 1.5 copy-start.11
  144.2 1.5 copy-start.30
  154.4 20.0 %copy-start.28 = (f32[640]{0:T(1024)S(1)}, f32[640]{0:T(1024)}, u32[]{:S(2)}) copy-start(f32[640]{0:T(1024)} %param.24) | copy-start | bytes 7684
Sparse Core Ops, SparseCore 0:
  10.1 37.6 all-gather.4
  95.6 34.7 all-gather.6
where the time goes:
time: 242 us; the launch traced here: 241 us
  blocking collectives  98.4 us (41%)
  waiting for transfers between devices  33.8 us (14%)
  local copies, waits for them, and re-layouts  32.7 us (14%)
  matrix products  30.8 us (13%)
  other arithmetic  28 us (12%)
  between operations  13.9 us (6%)
  starting transfers between devices  3.23 us (1%)
    all_to_all x1, blocking collectives, summed_on_arrival(): lax.all_to_all(pieces, axis, split_axis=0, concat_axis=0, tiled=True)  49.8 us
    all_gather x3, blocking collectives, entering(): lax.all_gather(part.astype(kind), axis)  31.2 us
    all_gather x1, waiting for transfers between devices, on_device(): normed = lax.all_gather(own_normed, 'head', axis=0, tiled=True)  29.7 us
    all_to_all x1, blocking collectives, from_everyone(): lax.all_to_all(jnp.broadcast_to(array[None], (length, *array.shape)), axi...  17.4 us
    unnamed x66, local copies, waits for them, and re-layouts  10.6 us
    dot_general x1, matrix products, on_device(): jnp.dot(normed, joined_proj, preferred_element_type=jnp.float32)  8.94 us
    dot_general x1, matrix products, on_device(): jnp.dot(normed_out, out_proj, preferred_element_type=jnp.float32)  6.16 us
    dot_general x1, matrix products, on_device(): outer_part = jnp.dot(normed, outer_proj, preferred_element_type=jnp.float32)  5.31 us
  transfers between devices with their start and end apart: 3, of which 2 were waited for; matrix products, arithmetic and copies ran while one was open for 9% of the time, Pallas kernels for 0%

commit v1 on v0

--- a/solution.py
+++ b/solution.py
@@ -99,7 +99,8 @@
     kernel_size = kernel_x.shape[0]
     joined_proj = inner_proj.reshape(model_width, 2 * local_width)
     own_normed = row_norm(tokens, pre_gain).astype(jnp.bfloat16)
-    normed = lax.all_gather(own_normed, "head", axis=0, tiled=True)
+    repeated = jnp.stack([own_normed] * lax.axis_size("head"))
+    normed = jnp.concatenate(lax.all_to_all(repeated, "head", 0, 0), axis=0)
     inner_part = jnp.dot(normed, joined_proj, preferred_element_type=jnp.float32)
     outer_part = jnp.dot(normed, outer_proj, preferred_element_type=jnp.float32)
     projected = jnp.concatenate([inner_part, outer_part], axis=1)

time: 242 us -> 259 us (1.070)
  waiting for transfers between devices: 33.8 us -> 41.5 us
  starting transfers between devices: 3.23 us -> 9.62 us
    all_to_all x0 -> x1, waiting for transfers between devices: none -> 38 us  [on_device(): normed = jnp.concatenate(lax.all_to_all(repeated, 'head', 0, 0), axis=0)]
    all_gather x1 -> x0, waiting for transfers between devices: 29.7 us -> none  [on_device(): normed = lax.all_gather(own_normed, 'head', axis=0, tiled=True)]
    all_to_all x0 -> x1, starting transfers between devices: none -> 7.6 us  [on_device(): normed = jnp.concatenate(lax.all_to_all(repeated, 'head', 0, 0), axis=0)]
    unnamed x66 -> x68, local copies, waits for them, and re-layouts: 10.6 us -> 10.4 us
  transfers between devices with their start and end apart: 3 -> 3, of which waited for: 2 -> 2; matrix products, arithmetic and copies ran while one was open for 9% -> 8% of each run, Pallas kernels for 0% -> 0%
where the time goes in v1:
time: 259 us; the launch traced here: 258 us
  blocking collectives  100 us (39%)
  waiting for transfers between devices  41.5 us (16%)
  local copies, waits for them, and re-layouts  34.9 us (13%)
  matrix products  30 us (12%)
  other arithmetic  27.9 us (11%)
  between operations  13.9 us (5%)
  starting transfers between devices  9.62 us (4%)
    all_to_all x1, blocking collectives, summed_on_arrival(): lax.all_to_all(pieces, axis, split_axis=0, concat_axis=0, tiled=True)  49.8 us
    all_to_all x1, waiting for transfers between devices, on_device(): normed = jnp.concatenate(lax.all_to_all(repeated, 'head', 0, 0), axis=0)  38 us
    all_gather x3, blocking collectives, entering(): lax.all_gather(part.astype(kind), axis)  33.2 us
    all_to_all x1, blocking collectives, from_everyone(): lax.all_to_all(jnp.broadcast_to(array[None], (length, *array.shape)), axi...  17.4 us
    unnamed x68, local copies, waits for them, and re-layouts  10.4 us
    dot_general x1, matrix products, on_device(): jnp.dot(normed, joined_proj, preferred_element_type=jnp.float32)  7.94 us
    all_to_all x1, starting transfers between devices, on_device(): normed = jnp.concatenate(lax.all_to_all(repeated, 'head', 0, 0), axis=0)  7.6 us
    dot_general x1, matrix products, on_device(): jnp.dot(normed_out, out_proj, preferred_element_type=jnp.float32)  6.16 us
  transfers between devices with their start and end apart: 3, of which 2 were waited for; matrix products, arithmetic and copies ran while one was open for 8% of the time, Pallas kernels for 0%

profile of v1, /device:TPU:1, one launch (start us, length us, event | category | flops | bytes accessed | tf_op | source)
XLA Modules:
  0.0 258.2 jit_solution(9409515362096897362)
XLA Ops:
  6.5 1.4 fusion.16
  7.9 1.2 fusion.18
  9.2 2.3 stack.2
  11.5 7.6 %all-to-all-start = ((bf16[8,96,2560]{2,1,0:T(8,128)(2,1)}), bf16[8,96,2560]{2,1,0:T(8,128)(2,1)}, u32[]{:S(2)}, u32[]{:S(2)}) async-start(bf16[8,96,2560]{2,1,0:T(8,128)(2,1)} %stack.2), calls=%async_computation | async-start | bytes 7864320 | tf_op jit(solution)/shard_map/all_to_all | solution.py:103
  19.1 6.7 %copy.137 = bf16[320,8,2,640]{3,1,2,0:T(8,128)(2,1)} copy(bf16[320,8,2,640]{3,2,1,0:T(2,128)(2,1)} %bitcast.168) | data formatting | bytes 13107200
  25.9 0.5 iota_compare_fusion.1
  26.4 0.6 pad_maximum_fusion.3
  27.1 38.0 %all-to-all-done = bf16[8,96,2560]{2,1,0:T(8,128)(2,1)} async-done(((bf16[8,96,2560]{2,1,0:T(8,128)(2,1)}), bf16[8,96,2560]{2,1,0:T(8,128)(2,1)}, u32[]{:S(2)}, u32[]{:S(2)}) %all-to-all-start) | async-done | bytes 3932192 | tf_op jit(solution)/shard_map/all_to_all | solution.py:103
  65.1 5.5 %fusion.66 = (bf16[768,336]{0,1:T(8,128)(2,1)}, f32[768,336]{0,1:T(8,128)}) fusion(bf16[768,2560]{1,0:T(8,128)(2,1)} %bitcast, bf16[2560,336]{0,1:T(8,128)(2,1)} %param.16), kind=kOutput, calls=%fused_computation.144 | convolution fusion | flops 1321463808 | bytes 7200768 | tf_op jit(solution)/shard_map/dot_general | solution.py:105
  70.6 7.9 %convolution_convert_fusion.1 = bf16[768,1280]{1,0:T(8,128)(2,1)} fusion(bf16[768,2560]{1,0:T(8,128)(2,1)} %bitcast, bf16[2560,1280]{1,0:T(8,128)(2,1)S(1)} %bitcast.169), kind=kOutput, calls=%fused_computation.9 | convolution fusion | flops 5034147840 | bytes 12451840 | tf_op jit(solution)/shard_map/dot_general | solution.py:104
  78.5 2.1 copy.111
  80.6 1.5 pad_maximum_fusion.2
  82.2 0.1 copy-done.5
  82.3 1.2 pad_maximum_fusion.1
  83.5 1.0 slice.213
  84.5 0.1 broadcast_multiply_fusion
  84.7 1.7 reduce-window.6
  86.4 0.2 slice_reduce_fusion
  86.8 0.1 copy.121
  87.1 2.0 collective-permute-start
  89.1 0.6 bitcast_exponential_fusion
  89.8 0.7 copy.124
  90.5 0.6 copy.123
  91.1 0.7 copy.125
  91.8 5.0 %multiply_convert_fusion.2 = bf16[768,896]{1,0:T(8,128)(2,1)S(1)} fusion(bf16[768,896]{1,0:T(8,128)(2,1)} %pad_maximum_fusion.1, bf16[3,896]{1,0:T(4,128)(2,1)S(1)} %collective-permute-done, f32[896]{0:T(1024)S(1)} %get-tuple-element.6, f32[896]{0:T(1024)S(1)} %get-tuple-element.7, f32[896]{0:T(1024)S(1)} %get-tuple-element.8, f32[896]{0:T(1024)S(1)} %get-tuple-element.5, ...), kind=kLoop, calls=%fused_computation.10 | loop fusion | flops 17891328 | bytes 2775808 | tf_op jit(solution)/shard_map/convert_element_type | solution.py:123
  96.8 0.7 fusion.65
  97.5 1.1 slice.210
  98.5 2.3 copy.112
  100.8 3.8 %reshape.243 = bf16[3,256,10,64]{1,0,3,2:T(4,128)(2,1)} reshape(bf16[768,640]{0,1:T(8,128)(2,1)} %copy.112) | data formatting | bytes 1966080 | tf_op jit(solution)/shard_map/reshape | solution.py:125
  104.6 1.8 fusion.19
  106.4 2.8 %convolution_bitcast_fusion = f32[4,10,64,128]{3,0,2,1:T(4,128)S(1)} fusion(f32[3,10,64,128]{3,2,1,0:T(8,128)S(1)} %fusion.19, f32[10,3]{1,0:T(8,128)S(1)} %copy-done.15, f32[10,4]{1,0:T(8,128)S(1)} %copy-done.14, pred[4,3]{1,0:T(4,128)(4,1)S(1)} %copy-done.28), kind=kOutput, calls=%fused_computation.26 | convolution fusion | flops 11796840 | bytes 2294052 | tf_op jit(solution)/shard_map/hce,ehpn->chpn/dot_general | solution.py:161
  109.2 1.1 copy-done.2
  110.3 0.3 slice.387
  110.7 0.7 copy.128
  111.4 0.6 iota_compare_fusion
  112.0 1.4 slice_exponential_fusion
  113.4 13.8 %all-gather = bf16[8,1,10]{2,1,0:T(2,128)(2,1)S(1)} all-gather(bf16[1,1,10]{2,1,0:T(2,128)(2,1)S(1)} %slice_bitcast_fusion.5), channel_id=1, replica_groups=mesh['seq_0'=4,'seq_1'=8,'head'=8] {'seq_1'}, dimensions={0}, use_global_device_ids=true | all-gather | bytes 180 | tf_op jit(solution)/shard_map/all_gather | solution.py:31
  127.2 0.6 fusion.39
  127.8 0.6 convert_bitcast_fusion
  128.4 8.8 %all-gather.1 = bf16[4,1,10]{2,1,0:T(2,128)(2,1)} all-gather(bf16[1,1,10]{2,1,0:T(2,128)(2,1)S(1)} %get-tuple-element.17), channel_id=1, replica_groups=mesh['seq_0'=4,'seq_1'=8,'head'=8] {'seq_0'}, dimensions={0}, use_global_device_ids=true | all-gather | bytes 100 | tf_op jit(solution)/shard_map/all_gather | solution.py:31
  137.1 0.6 copy.115
  137.8 0.8 copy.127
  138.6 1.4 copy.119
  140.0 0.6 copy.117
  140.6 0.6 exponential_bitcast_fusion
  141.2 0.7 fusion.49
  141.9 2.1 fusion.67
  144.0 3.5 %all-gather.4.cloned.1.call-done = bf16[8,10,64,128]{3,2,1,0:T(8,128)(2,1)} async-done(((bf16[1,10,64,128]{3,2,1,0:T(8,128)(2,1)}), bf16[8,10,64,128]{3,2,1,0:T(8,128)(2,1)}) %all-gather.4.cloned.1.call-update) | async-done | bytes 1310736 | tf_op jit(solution)/shard_map/all_gather | solution.py:31
  147.5 1.9 fusion.28
  149.4 10.7 %all_gather.19 = bf16[4,10,64,128]{3,2,1,0:T(8,128)(2,1)S(1)} all-gather(bf16[1,10,64,128]{3,2,1,0:T(8,128)(2,1)S(1)} %fusion.28), channel_id=1, replica_groups=mesh['seq_0'=4,'seq_1'=8,'head'=8] {'seq_0'}, dimensions={0}, use_global_device_ids=true | all-gather | bytes 819200 | tf_op jit(solution)/shard_map/all_gather | solution.py:31
  160.2 1.0 add_bitcast_fusion
  161.1 0.4 slice_add_fusion
  161.6 0.9 fusion.21
  162.6 0.3 copy-done.7
  162.9 0.2 copy-done.8
  163.1 2.7 %fusion.8 = f32[3,256,10,64]{1,3,2,0:T(8,128)S(1)} fusion(f32[3,256,10,64]{1,3,2,0:T(8,128)S(1)} %fusion.21, f32[3,10,256]{2,1,0:T(8,128)S(1)} %copy-done.12, f32[3,10,256]{2,1,0:T(8,128)S(1)} %copy-done.10, f32[3,256,256]{2,1,0:T(8,128)S(1)} %copy-done.8, pred[256,256]{1,0:T(8,128)(4,1)S(1)} %copy-done.9, f32[10]{0:T(128)S(1)} %copy-done.31, ...), kind=kOutput, calls=%fused_computation.16 | convolution fusion | flops 265912320 | bytes 5859368 | tf_op jit(solution)/shard_map/chts,cshp->cthp/dot_general | solution.py:143
  165.8 1.4 copy.130
  167.2 1.8 copy.138
  168.9 2.8 %copy.131 = f32[768,640]{1,0:T(8,128)} copy(f32[768,640]{0,1:T(8,128)} %bitcast.167) | data formatting | bytes 3932160 | tf_op jit(solution)/shard_map/reshape | solution.py:187
  171.8 2.5 multiply_reduce_fusion
  174.3 17.4 %all_to_all.16 = f32[8,1,768]{2,1,0:T(1,128)S(1)} all-to-all(f32[8,1,768]{2,1,0:T(1,128)S(1)} %broadcast_in_dim.36), channel_id=1, replica_groups=mesh['seq_0'=4,'seq_1'=8,'head'=8] {'head'}, dimensions={0} | all-to-all | bytes 49152 | tf_op jit(solution)/shard_map/all_to_all | solution.py:48
  191.8 6.2 %convolution_convert_fusion = bf16[768,2560]{1,0:T(8,128)(2,1)S(1)} fusion(bf16[640,2560]{1,0:T(8,128)(2,1)S(1)} %copy-done, f32[640]{0:T(1024)S(1)} %copy-done.29, f32[768]{0:T(1024)S(1)} %add_rsqrt_fusion, f32[768,640]{1,0:T(8,128)} %copy.131, bf16[768,1280]{1,0:T(8,128)(2,1)} %convolution_convert_fusion.1), kind=kOutput, calls=%fused_computation.1 | convolution fusion | flops 2522972160 | bytes 10163712 | tf_op jit(solution)/shard_map/dot_general | solution.py:195
  197.9 49.8 %all_to_all.17 = bf16[8,96,2560]{2,1,0:T(8,128)(2,1)} all-to-all(bf16[8,96,2560]{2,1,0:T(8,128)(2,1)S(1)} %bitcast.170), channel_id=1, replica_groups=mesh['seq_0'=4,'seq_1'=8,'head'=8] {'head'}, dimensions={0} | all-to-all | bytes 7864320 | tf_op jit(solution)/shard_map/all_to_all | solution.py:65
  247.7 3.6 %reduce_sum.42 = bf16[96,2560]{1,0:T(8,128)(2,1)} reduce(bf16[8,96,2560]{2,1,0:T(8,128)(2,1)} %all_to_all.17, bf16[]{:T(256)} %constant.60.clone.1), dimensions={0}, to_apply=%region_6.7 | reduce | flops 1720320 | bytes 4423682 | tf_op jit(solution)/shard_map/reduce_sum | solution.py:66
  (86 shorter events, 0.8 us)
Async XLA Ops:
  6.5 185.2 %copy-start = (bf16[640,2560]{1,0:T(8,128)(2,1)S(1)}, bf16[640,2560]{1,0:T(8,128)(2,1)}, u32[]{:S(2)}) copy-start(bf16[640,2560]{1,0:T(8,128)(2,1)} %param.25) | copy-start | bytes 9830404
  11.5 53.6 %all-to-all-start = ((bf16[8,96,2560]{2,1,0:T(8,128)(2,1)}), bf16[8,96,2560]{2,1,0:T(8,128)(2,1)}, u32[]{:S(2)}, u32[]{:S(2)}) async-start(bf16[8,96,2560]{2,1,0:T(8,128)(2,1)} %stack.2), calls=%async_computation | async-start | bytes 7864320 | tf_op jit(solution)/shard_map/all_to_all | solution.py:103
  19.1 128.5 %all-gather.4.cloned.1.call-start = ((), (), s32[]{:S(2)}) async-start(), calls=%async_computation.3 | async-start | bytes 1474560 | tf_op jit(solution)/shard_map/all_gather | solution.py:31
  19.1 7.3 %copy-start.17 = (f32[4,640]{1,0:T(4,128)S(1)}, f32[4,640]{1,0:T(4,128)}, u32[]{:S(2)}) copy-start(f32[4,640]{1,0:T(4,128)} %param.17) | copy-start | bytes 30724
  19.1 7.3 %copy-start.23 = (f32[4,256]{1,0:T(4,128)S(1)}, f32[4,256]{1,0:T(4,128)}, u32[]{:S(2)}) copy-start(f32[4,256]{1,0:T(4,128)} %param.18) | copy-start | bytes 12292
  19.1 7.3 %copy-start.24 = (f32[640]{0:T(1024)S(1)}, f32[640]{0:T(1024)}, u32[]{:S(2)}) copy-start(f32[640]{0:T(1024)} %param.19) | copy-start | bytes 7684
  19.1 7.3 %copy-start.26 = (f32[256]{0:T(256)S(1)}, f32[256]{0:T(256)}, u32[]{:S(2)}) copy-start(f32[256]{0:T(256)} %param.20) | copy-start | bytes 3076
  19.1 7.9 %copy-start.30 = (f32[10]{0:T(128)S(1)}, f32[10]{0:T(128)}, u32[]{:S(2)}) copy-start(f32[10]{0:T(128)} %param.22) | copy-start | bytes 124
  65.1 5.5 %copy-start.4 = (bf16[320,8,2,640]{3,1,2,0:T(8,128)(2,1)S(1)}, bf16[320,8,2,640]{3,1,2,0:T(8,128)(2,1)}, u32[]{:S(2)}) copy-start(bf16[320,8,2,640]{3,1,2,0:T(8,128)(2,1)} %copy.137) | copy-start | bytes 19660804
  80.6 1.6 copy-start.1
  80.6 1.7 copy-start.5
  82.3 2.2 copy-start.27
  87.1 4.7 %copy-start.16 = (f32[3,10]{1,0:T(4,128)}, f32[3,10]{1,0:T(4,128)S(1)}, u32[]{:S(2)}) copy-start(f32[3,10]{1,0:T(4,128)S(1)} %reduce_window_sum.36) | copy-start | bytes 364
  87.1 4.7 %collective-permute-start = (bf16[3,896]{1,0:T(4,128)(2,1)}, bf16[3,896]{1,0:T(4,128)(2,1)S(1)}, u32[]{:S(2)}, u32[]{:S(2)}) collective-permute-start(bf16[3,896]{1,0:T(4,128)(2,1)} %pad_maximum_fusion.2), channel_id=1, source_target_pairs={{0,8},{8,16},{16,24},{24,32},{32,40},{40,48},{48,56},{56,64},{64,7... | collective-permute-start | bytes 16136 | tf_op jit(solution)/shard_map/ppermute | solution.py:16
  104.5 1.8 copy-start.14
  104.6 1.8 copy-start.15
  104.6 1.8 copy-start.28
  109.2 1.1 copy-start.2
  127.2 10.6 %copy-start.13 = (bf16[8,1,10]{2,1,0:T(2,128)(2,1)}, bf16[8,1,10]{2,1,0:T(2,128)(2,1)S(1)}, u32[]{:S(2)}) copy-start(bf16[8,1,10]{2,1,0:T(2,128)(2,1)S(1)} %all-gather) | copy-start | bytes 484
  137.8 22.3 %copy-start.18 = (f32[10]{0:T(128)S(1)}, f32[10]{0:T(128)}, u32[]{:S(2)}) copy-start(f32[10]{0:T(128)} %get-tuple-element.18) | copy-start | bytes 124
  137.8 22.3 %copy-start.19 = (f32[10]{0:T(128)S(1)}, f32[10]{0:T(128)}, u32[]{:S(2)}) copy-start(f32[10]{0:T(128)} %get-tuple-element.19) | copy-start | bytes 124
  137.8 22.3 %copy-start.20 = (f32[10]{0:T(128)S(1)}, f32[10]{0:T(128)}, u32[]{:S(2)}) copy-start(f32[10]{0:T(128)} %get-tuple-element.20) | copy-start | bytes 124
  137.8 22.3 %copy-start.21 = (f32[10]{0:T(128)S(1)}, f32[10]{0:T(128)}, u32[]{:S(2)}) copy-start(f32[10]{0:T(128)} %get-tuple-element.21) | copy-start | bytes 124
  137.8 22.3 %copy-start.22 = (f32[10]{0:T(128)S(1)}, f32[10]{0:T(128)}, u32[]{:S(2)}) copy-start(f32[10]{0:T(128)} %get-tuple-element.22) | copy-start | bytes 124
  140.6 19.5 %copy-start.25 = (f32[10]{0:T(128)S(1)}, f32[10]{0:T(128)}, u32[]{:S(2)}) copy-start(f32[10]{0:T(128)} %get-tuple-element.9) | copy-start | bytes 124
  147.5 12.6 %copy-start.6 = (bf16[8,10,64,128]{3,2,1,0:T(8,128)(2,1)S(1)}, bf16[8,10,64,128]{3,2,1,0:T(8,128)(2,1)}, u32[]{:S(2)}) copy-start(bf16[8,10,64,128]{3,2,1,0:T(8,128)(2,1)} %all-gather.4.cloned.1.call-done) | copy-start | bytes 3932164
  147.5 13.6 %copy-start.3 = (f32[4,10,64,128]{3,0,2,1:T(4,128)S(1)}, f32[4,10,64,128]{3,0,2,1:T(4,128)}, u32[]{:S(2)}) copy-start(f32[4,10,64,128]{3,0,2,1:T(4,128)} %copy-done.2) | copy-start | bytes 3932164
  161.6 1.3 copy-start.7
  161.6 1.5 copy-start.8
  161.6 1.5 copy-start.9
  161.6 1.5 copy-start.10
  161.6 1.5 copy-start.11
  161.6 1.5 copy-start.12
  161.6 1.5 copy-start.31
  171.8 20.0 %copy-start.29 = (f32[640]{0:T(1024)S(1)}, f32[640]{0:T(1024)}, u32[]{:S(2)}) copy-start(f32[640]{0:T(1024)} %param.24) | copy-start | bytes 7684
Sparse Core Ops, SparseCore 0:
  111.5 35.9 all-gather.3
